TPU v7x, 32 devices: a whole 2x2x4 slice. The times are simulated.
32 devices in a mesh: rows: 8 (over z, x), cols: 4 (over y, core).
Axes of the slice: x: 2, y: 2, z: 4, core: 2. Of those that a mesh axis runs over, the one named last changes fastest.
Arguments:
- left_features: bfloat16 [2, 96, 512, 256], P(None, 'rows', 'cols'), may hold values from -6 to 6
- right_features: bfloat16 [2, 96, 512, 256], P(None, 'rows', 'cols'), may hold values from -6 to 6
- conv_weight: bfloat16 [3, 3, 256, 256], replicated, may hold values from -0.125 to 0.125
- conv_bias: float32 [256], replicated, may hold values from -3 to 3
Outputs:
- pyramid_out: float32 [2, 96, 512, 480], P(None, 'rows', 'cols')
All inputs are finite; a program needn't handle non-finite values.
Results may differ from a plain program's by a relative error of at most 0.0012.
Values may be sent and summed in bfloat16 or wider, within the bound.
A program may use at most 64 MiB of HBM per device.

v0:
```python
import functools
import math

import jax
import jax.numpy as jnp
from jax import lax
from jax.experimental import pallas as pl
from jax.experimental.pallas import tpu as pltpu
from jax.sharding import PartitionSpec as P

DISP = 256
LEVELS = 4


def padded_2(cells, sides, width):
    for axis, dim in sides:
        count = lax.axis_size(axis)
        ends = count - 1
        head = lax.slice_in_dim(cells, 0, width, axis=dim)
        tail = lax.slice_in_dim(cells, cells.shape[dim] - width, cells.shape[dim], axis=dim)
        cells = jnp.concatenate(
            [
                lax.ppermute(tail, axis, [(i, (i + 1) % count) for i in range(ends)]),
                cells,
                lax.ppermute(head, axis, [((i + 1) % count, i) for i in range(ends)]),
            ],
            axis=dim,
        )
    return cells


def shifted(value, axis, steps):
    count = lax.axis_size(axis)
    leading, last = (max(0, -steps), min(count, count - steps))
    return lax.ppermute(value, axis, [(source, source + steps) for source in range(leading, last)])


def encode(padded, conv_weight, conv_bias):
    batch = padded.shape[0]
    height = padded.shape[1] - 2
    breadth = padded.shape[2] - 2
    channels = padded.shape[3]
    total = jnp.zeros((batch * height * breadth, channels), jnp.float32)
    for row_tap in range(3):
        for col_tap in range(3):
            window = padded[:, row_tap : row_tap + height, col_tap : col_tap + breadth].reshape(
                -1, channels
            )
            total = total + jnp.dot(
                window, conv_weight[row_tap, col_tap], preferred_element_type=jnp.float32
            )
    centre = padded[:, 1:-1, 1:-1].reshape(-1, channels).astype(jnp.float32)
    encoded = centre + jax.nn.relu(total + conv_bias)
    return encoded.astype(jnp.bfloat16).reshape(batch, height, breadth, channels)


def pooling(span_count, level_count):
    lines = []
    entry = lax.broadcasted_iota(jnp.int32, (1, span_count), 1)
    for level in range(1, level_count):
        group = lax.broadcasted_iota(jnp.int32, (span_count >> level, 1), 0)
        lines.append(jnp.where((entry >> level) == group, 0.5**level, 0.0))
    return jnp.concatenate(lines, axis=0).astype(jnp.bfloat16)


def skewed(scores, span_count, scratch):
    breadth = scores.shape[1]
    lane = lax.broadcasted_iota(jnp.int32, (1, breadth), 1)
    steps = breadth - 1 - lane
    bit = breadth // 2
    while bit >= 8:
        keep = span_count + bit
        scores = jnp.where((steps & bit) != 0, scores[bit : bit + keep], scores[:keep])
        bit //= 2
    for stage, bit in enumerate((4, 2, 1)):
        keep = span_count + (8 if bit > 1 else 0)
        scratch[stage, : span_count + 8] = scores
        scores = jnp.where((steps & bit) != 0, scratch[stage, pl.ds(bit, keep)], scores[:keep])
    return scores


def correlate_kernel(span_count, scale, left_ref, *refs):
    right_refs, pool_ref, out_ref, scratch = refs[:-3], refs[-3], refs[-2], refs[-1]
    rows = left_ref.shape[0]
    pool = pool_ref[...]
    breadth = left_ref.shape[1]
    for pair in range(0, rows, 2):
        volumes = []
        for row in range(pair, min(pair + 2, rows)):
            query = left_ref[row]
            scores = jnp.concatenate(
                [
                    lax.dot_general(
                        ref[row], query, (((1,), (1,)), ((), ())), preferred_element_type=jnp.float32
                    )
                    for ref in right_refs
                ],
                axis=0,
            )
            volume = skewed(scores, span_count, scratch.at[row]) * scale
            out_ref[row, :span_count] = volume
            volumes.append(volume)
        volume = jnp.concatenate(volumes, axis=1)
        high = volume.astype(jnp.bfloat16)
        low = (volume - high.astype(jnp.float32)).astype(jnp.bfloat16)
        pooled = jnp.dot(pool, high, preferred_element_type=jnp.float32) + jnp.dot(
            pool, low, preferred_element_type=jnp.float32
        )
        for index in range(len(volumes)):
            out_ref[pair + index, span_count:] = pooled[:, index * breadth : (index + 1) * breadth]


def correlate(left, rights, span_count, level_count, block):
    rows, breadth, channels = left.shape
    pool = pooling(span_count, level_count)
    width = span_count + pool.shape[0]
    part = pl.BlockSpec((block, breadth, channels), lambda i: (i, 0, 0))
    return pl.pallas_call(
        functools.partial(correlate_kernel, span_count, 1.0 / math.sqrt(channels)),
        grid=(rows // block,),
        out_shape=jax.ShapeDtypeStruct((rows, width, breadth), jnp.float32),
        in_specs=[part] * (1 + len(rights)) + [pl.BlockSpec(pool.shape, lambda i: (0, 0))],
        out_specs=pl.BlockSpec((block, width, breadth), lambda i: (i, 0, 0)),
        scratch_shapes=[pltpu.VMEM((block, 3, span_count + 16, breadth), jnp.float32)],
        cost_estimate=pl.CostEstimate(
            flops=2 * rows * breadth * (len(rights) * breadth * channels + 2 * span_count * 256),
            bytes_accessed=rows * breadth * (2 * channels * (1 + len(rights)) + 4 * width),
            transcendentals=0,
        ),
    )(left, *rights, pool)


def shards(left_features, right_features, conv_weight, conv_bias):
    batch, height, breadth, channels = left_features.shape
    left_pad, right_pad = (
        padded_2(left_features, (("rows", 1), ("cols", 2)), 1),
        padded_2(right_features, (("rows", 1), ("cols", 2)), 1),
    )
    left_out = encode(left_pad, conv_weight, conv_bias)
    right_out = encode(right_pad, conv_weight, conv_bias)
    flip = jnp.eye(breadth, dtype=jnp.bfloat16)[::-1]
    right_out = jnp.einsum("xy,bhyc->bhxc", flip, right_out)
    hops = DISP // breadth
    count = lax.axis_size("cols")
    if hops == 2 and count % 2 == 0:
        far = shifted(right_out, "cols", 2)
        pairs = range(0, count, 2)
        own = lax.ppermute(right_out, "cols", [(i, i + 1) for i in pairs])
        back = lax.ppermute(far, "cols", [(i + 1, i) for i in pairs])
        odd = lax.rem(lax.axis_index("cols"), 2) == 1
        pieces = [right_out, jnp.where(odd, own, back), far]
    else:
        pieces = [right_out] + [shifted(right_out, "cols", step) for step in range(1, hops + 1)]
    rows_total = batch * height
    flat = [piece.reshape(rows_total, breadth, channels) for piece in pieces]
    out = correlate(
        left_out.reshape(rows_total, breadth, channels), flat, DISP, LEVELS, math.gcd(rows_total, 4)
    )
    return jnp.swapaxes(out, 1, 2).reshape(batch, height, breadth, -1)


def solution(mesh):
    return jax.shard_map(
        shards,
        mesh=mesh,
        in_specs=(P(None, "rows", "cols", None), P(None, "rows", "cols", None), P(), P()),
        out_specs=P(None, "rows", "cols", None),
        check_vma=False,
    )
```

profile of v0, /device:TPU:21, one launch (start us, length us, event | category | flops | bytes accessed | tf_op | source)
XLA Modules:
  0.0 117.2 jit_solution(15393362273882254453)
XLA Ops:
  1.1 3.1 %collective-permute-start = (bf16[2,1,128,256]{3,2,1,0:T(8,128)(2,1)S(1)}, bf16[2,1,128,256]{3,2,1,0:T(8,128)(2,1)S(1)}, u32[]{:S(2)}, u32[]{:S(2)}) collective-permute-start(bf16[2,1,128,256]{3,2,1,0:T(8,128)(2,1)S(1)} %get-tuple-element.36), channel_id=1, source_target_pairs={{0,4},{4,8},{8,12},{12,16},{16,20},{20,24},{24,28},{1,5},{5,9},{9,... | collective-permute-start | bytes 393224 | tf_op jit(solution)/shard_map/ppermute | solution.py:23
  4.2 3.1 %collective-permute-start.1 = (bf16[2,1,128,256]{3,2,1,0:T(8,128)(2,1)S(1)}, bf16[2,1,128,256]{3,2,1,0:T(8,128)(2,1)S(1)}, u32[]{:S(2)}, u32[]{:S(2)}) collective-permute-start(bf16[2,1,128,256]{3,2,1,0:T(8,128)(2,1)S(1)} %get-tuple-element.35), channel_id=1, source_target_pairs={{4,0},{8,4},{12,8},{16,12},{20,16},{24,20},{28,24},{5,1},{9,5},{13... | collective-permute-start | bytes 393224 | tf_op jit(solution)/shard_map/ppermute | solution.py:25
  7.3 1.7 %fusion.66 = (bf16[2,1,128,256]{3,2,1,0:T(8,128)(2,1)}, bf16[2,1,128,256]{3,2,1,0:T(8,128)(2,1)}) fusion(bf16[2,12,128,256]{3,2,1,0:T(8,128)(2,1)} %param.5), kind=kLoop, calls=%fused_computation.121 | loop fusion | bytes 524288 | tf_op jit(solution)/shard_map/slice | solution.py:19
  9.0 2.2 %collective-permute-start.4 = (bf16[2,1,128,256]{3,2,1,0:T(8,128)(2,1)}, bf16[2,1,128,256]{3,2,1,0:T(8,128)(2,1)S(1)}, u32[]{:S(2)}, u32[]{:S(2)}) collective-permute-start(bf16[2,1,128,256]{3,2,1,0:T(8,128)(2,1)} %get-tuple-element.31), channel_id=1, source_target_pairs={{0,4},{4,8},{8,12},{12,16},{16,20},{20,24},{24,28},{1,5},{5,9},{9,... | collective-permute-start | bytes 393224 | tf_op jit(solution)/shard_map/ppermute | solution.py:23
  11.2 4.0 %collective-permute-start.5 = (bf16[2,1,128,256]{3,2,1,0:T(8,128)(2,1)}, bf16[2,1,128,256]{3,2,1,0:T(8,128)(2,1)S(1)}, u32[]{:S(2)}, u32[]{:S(2)}) collective-permute-start(bf16[2,1,128,256]{3,2,1,0:T(8,128)(2,1)} %get-tuple-element.30), channel_id=1, source_target_pairs={{4,0},{8,4},{12,8},{16,12},{20,16},{24,20},{28,24},{5,1},{9,5},{13... | collective-permute-start | bytes 393224 | tf_op jit(solution)/shard_map/ppermute | solution.py:25
  16.7 1.3 %collective-permute-start.2 = (bf16[2,14,1,256]{3,2,1,0:T(2,128)(2,1)S(1)}, bf16[2,14,1,256]{3,2,1,0:T(2,128)(2,1)S(1)}, u32[]{:S(2)}, u32[]{:S(2)}) collective-permute-start(bf16[2,14,1,256]{3,2,1,0:T(2,128)(2,1)S(1)} %get-tuple-element.25), channel_id=1, source_target_pairs={{0,1},{1,2},{2,3},{4,5},{5,6},{6,7},{8,9},{9,10},{10,11},{12,13},{... | collective-permute-start | bytes 43016 | tf_op jit(solution)/shard_map/ppermute | solution.py:23
  18.0 4.3 %collective-permute-start.3 = (bf16[2,14,1,256]{3,2,1,0:T(2,128)(2,1)S(1)}, bf16[2,14,1,256]{3,2,1,0:T(2,128)(2,1)S(1)}, u32[]{:S(2)}, u32[]{:S(2)}) collective-permute-start(bf16[2,14,1,256]{3,2,1,0:T(2,128)(2,1)S(1)} %get-tuple-element.26), channel_id=1, source_target_pairs={{1,0},{2,1},{3,2},{5,4},{6,5},{7,6},{9,8},{10,9},{11,10},{13,12},{... | collective-permute-start | bytes 43016 | tf_op jit(solution)/shard_map/ppermute | solution.py:25
  26.3 4.3 %collective-permute-start.7 = (bf16[2,14,1,256]{3,2,1,0:T(2,128)(2,1)S(1)}, bf16[2,14,1,256]{3,2,1,0:T(2,128)(2,1)S(1)}, u32[]{:S(2)}, u32[]{:S(2)}) collective-permute-start(bf16[2,14,1,256]{3,2,1,0:T(2,128)(2,1)S(1)} %get-tuple-element.21), channel_id=1, source_target_pairs={{1,0},{2,1},{3,2},{5,4},{6,5},{7,6},{9,8},{10,9},{11,10},{13,12},{... | collective-permute-start | bytes 43016 | tf_op jit(solution)/shard_map/ppermute | solution.py:25
  31.7 5.1 %pad_maximum_fusion.2 = (bf16[2,12,128,256]{3,2,1,0:T(8,128)(2,1)S(1)}, bf16[2,12,128,256]{3,2,1,0:T(8,128)(2,1)S(1)}, bf16[2,12,128,256]{3,2,1,0:T(8,128)(2,1)S...) fusion(bf16[2,14,128,256]{3,2,1,0:T(8,128)(2,1)S(1)} %constant_, ...), kind=kLoop, calls=%fused_computation.50 | loop fusion | flops 18874368 | bytes 11300864 | tf_op jit(solution)/shard_map/concatenate | solution.py:21
  41.7 1.8 %convolution_bitcast_fusion = bf16[2,12,128,256]{2,3,1,0:T(8,128)(2,1)} fusion(bf16[2,12,128,256]{3,2,1,0:T(8,128)(2,1)S(1)} %bitcast.112, bf16[128,128]{1,0:T(8,128)(2,1)S(1)} %rev.3), kind=kOutput, calls=%fused_computation.57 | convolution fusion | flops 201326592 | bytes 3178496 | tf_op jit(solution)/shard_map/xy,bhyc->bhxc/dot_general | solution.py:142
  44.8 1.5 %collective-permute-start.9 = (bf16[2,12,128,256]{2,3,1,0:T(8,128)(2,1)}, bf16[2,12,128,256]{2,3,1,0:T(8,128)(2,1)}, u32[]{:S(2)}, u32[]{:S(2)}) collective-permute-start(bf16[2,12,128,256]{2,3,1,0:T(8,128)(2,1)} %convolution_bitcast_fusion), channel_id=1, source_target_pairs={{0,2},{1,3},{4,6},{5,7},{8,10},{9,11},{12,14},{13,15},{16,18},{17,... | collective-permute-start | bytes 4718600 | tf_op jit(solution)/shard_map/ppermute | solution.py:35
  46.3 6.5 %pad_maximum_fusion.6 = (bf16[2,12,128,256]{3,2,1,0:T(8,128)(2,1)}, bf16[2,12,128,256]{3,2,1,0:T(8,128)(2,1)S(1)}, bf16[2,12,128,256]{3,2,1,0:T(8,128)(2,1)S(1)}...) fusion(bf16[2,14,128,256]{3,2,1,0:T(8,128)(2,1)S(1)} %constant_d, ...), kind=kLoop, calls=%fused_computation.54 | loop fusion | flops 18874368 | bytes 11300864 | tf_op jit(solution)/shard_map/concatenate | solution.py:21
  54.0 2.2 %convolution_add_fusion.9 = f32[3072,256]{1,0:T(8,128)} fusion(f32[3072,256]{1,0:T(8,128)S(1)} %convolution_add_fusion.10, bf16[3072,256]{1,0:T(8,128)(2,1)S(1)} %bitcast.117, bf16[3,3,256,256]{3,2,1,0:T(8,128)(2,1)S(1)} %copy-done.6), kind=kOutput, calls=%fused_computation.17 | convolution fusion | flops 403439616 | bytes 7995392 | tf_op jit(solution)/shard_map/dot_general | solution.py:49
  56.2 26.1 %collective-permute-done.9 = bf16[2,12,128,256]{2,3,1,0:T(8,128)(2,1)} collective-permute-done((bf16[2,12,128,256]{2,3,1,0:T(8,128)(2,1)}, bf16[2,12,128,256]{2,3,1,0:T(8,128)(2,1)}, u32[]{:S(2)}, u32[]{:S(2)}) %collective-permute-start.9) | collective-permute-done | bytes 1572896 | tf_op jit(solution)/shard_map/ppermute | solution.py:35
  82.3 5.9 %collective-permute-start.10 = (bf16[2,12,128,256]{2,3,1,0:T(8,128)(2,1)}, bf16[2,12,128,256]{2,3,1,0:T(8,128)(2,1)}, u32[]{:S(2)}, u32[]{:S(2)}) collective-permute-start(bf16[2,12,128,256]{2,3,1,0:T(8,128)(2,1)} %collective-permute-done.9), channel_id=1, source_target_pairs={{1,0},{3,2},{5,4},{7,6},{9,8},{11,10},{13,12},{15,14},{17,16},{19,... | collective-permute-start | bytes 4718600 | tf_op jit(solution)/shard_map/ppermute | solution.py:149
  88.2 2.2 %fusion.22 = f32[3072,256]{1,0:T(8,128)} fusion(bf16[3072,256]{1,0:T(8,128)(2,1)S(1)} %bitcast.101, bf16[3,3,256,256]{3,2,1,0:T(8,128)(2,1)S(1)} %copy-done.6), kind=kOutput, calls=%fused_computation.60 | convolution fusion | flops 402653184 | bytes 4849664 | tf_op jit(solution)/shard_map/dot_general | solution.py:49
  90.4 2.6 %copy.6 = bf16[2,12,128,256]{3,2,1,0:T(8,128)(2,1)} copy(bf16[2,12,128,256]{2,3,1,0:T(8,128)(2,1)} %convolution_bitcast_fusion) | data formatting | bytes 3145728 | tf_op jit(solution)/shard_map/xy,bhyc->bhxc/transpose | solution.py:142
  93.0 3.1 %convolution_add_fusion.8 = f32[3072,256]{1,0:T(8,128)S(1)} fusion(f32[3072,256]{1,0:T(8,128)} %convolution_add_fusion.9, bf16[3072,256]{1,0:T(8,128)(2,1)} %bitcast.99, bf16[3,3,256,256]{3,2,1,0:T(8,128)(2,1)} %param.6), kind=kOutput, calls=%fused_computation.16 | convolution fusion | flops 403439616 | bytes 7995392 | tf_op jit(solution)/shard_map/dot_general | solution.py:49
  96.2 1.6 %convolution_add_fusion.7 = f32[3072,256]{1,0:T(8,128)S(1)} fusion(f32[3072,256]{1,0:T(8,128)S(1)} %convolution_add_fusion.8, bf16[3072,256]{1,0:T(8,128)(2,1)S(1)} %bitcast.114, bf16[3,3,256,256]{3,2,1,0:T(8,128)(2,1)} %param.6), kind=kOutput, calls=%fused_computation.15 | convolution fusion | flops 403439616 | bytes 7995392 | tf_op jit(solution)/shard_map/dot_general | solution.py:49
  99.1 3.0 %fusion.11 = bf16[3072,256]{1,0:T(8,128)(2,1)} fusion(f32[3072,256]{1,0:T(8,128)S(1)} %copy-done, f32[3072,256]{1,0:T(8,128)S(1)} %fusion.26, f32[3072,256]{1,0:T(8,128)S(1)} %convolution_add_fusion.7, bf16[3072,256]{1,0:T(8,128)(2,1)S(1)} %bitcast.107, bf16[3072,256]{1,0:T(8,128)(2,1)S(1)} %bitcast.100, f32[256]{0:T(256)S(1)} %copy-done.7, ...), kind=kOutput, calls=%fused_computation.23 | convolution fusion | flops 408944640 | bytes 14287872 | tf_op jit(solution)/shard_map/dot_general | solution.py:49
  102.1 2.6 %copy.8 = bf16[2,12,128,256]{3,2,1,0:T(8,128)(2,1)} copy(bf16[2,12,128,256]{2,3,1,0:T(8,128)(2,1)} %collective-permute-done.9) | data formatting | bytes 3145728 | tf_op jit(solution)/shard_map/ppermute | solution.py:35
  104.7 1.6 %broadcast_select_fusion = bf16[2,12,128,256]{2,3,1,0:T(8,128)(2,1)S(1)} fusion(bf16[2,12,128,256]{2,3,1,0:T(8,128)(2,1)} %collective-permute-done.8, bf16[2,12,128,256]{2,3,1,0:T(8,128)(2,1)} %collective-permute-done.10, pred[]{:T(512)S(6)} %eq.46), kind=kLoop, calls=%fused_computation.56 | loop fusion | flops 786432 | bytes 4718593 | tf_op jit(solution)/shard_map/jit(_where)/select_n | solution.py:151
  106.3 1.6 %copy.7 = bf16[2,12,128,256]{3,2,1,0:T(8,128)(2,1)} copy(bf16[2,12,128,256]{2,3,1,0:T(8,128)(2,1)S(1)} %broadcast_select_fusion) | data formatting | bytes 3145728 | tf_op jit(solution)/shard_map/jit(_where)/select_n | solution.py:151
  107.8 9.3 %shard_map.46 = f32[24,480,128]{2,1,0:T(8,128)} custom-call(bf16[24,128,256]{2,1,0:T(8,128)(2,1)} %bitcast.109, bf16[24,128,256]{2,1,0:T(8,128)(2,1)} %bitcast.110, bf16[24,128,256]{2,1,0:T(8,128)(2,1)} %bitcast.113, bf16[24,128,256]{2,1,0:T(8,128)(2,1)} %bitcast.111, bf16[224,256]{1,0:T(8,128)(2,1)} %pad_maximum_fusion.8.refs_3_), custom_call_target="tpu_custom_call" | custom-call | flops 1409286144 | bytes 12189696 | tf_op jit(solution)/shard_map/pallas_call | solution.py:118
  (59 shorter events, 16.0 us)
Async XLA Ops:
  0.0 16.0 %copy-start.2 = (bf16[2,12,128,256]{3,2,1,0:T(8,128)(2,1)S(1)}, bf16[2,12,128,256]{3,2,1,0:T(8,128)(2,1)}, u32[]{:S(2)}) copy-start(bf16[2,12,128,256]{3,2,1,0:T(8,128)(2,1)} %param.4) | copy-start | bytes 4718596
  1.1 14.9 %collective-permute-start = (bf16[2,1,128,256]{3,2,1,0:T(8,128)(2,1)S(1)}, bf16[2,1,128,256]{3,2,1,0:T(8,128)(2,1)S(1)}, u32[]{:S(2)}, u32[]{:S(2)}) collective-permute-start(bf16[2,1,128,256]{3,2,1,0:T(8,128)(2,1)S(1)} %get-tuple-element.36), channel_id=1, source_target_pairs={{0,4},{4,8},{8,12},{12,16},{16,20},{20,24},{24,28},{1,5},{5,9},{9,... | collective-permute-start | bytes 393224 | tf_op jit(solution)/shard_map/ppermute | solution.py:23
  4.2 11.8 %collective-permute-start.1 = (bf16[2,1,128,256]{3,2,1,0:T(8,128)(2,1)S(1)}, bf16[2,1,128,256]{3,2,1,0:T(8,128)(2,1)S(1)}, u32[]{:S(2)}, u32[]{:S(2)}) collective-permute-start(bf16[2,1,128,256]{3,2,1,0:T(8,128)(2,1)S(1)} %get-tuple-element.35), channel_id=1, source_target_pairs={{4,0},{8,4},{12,8},{16,12},{20,16},{24,20},{28,24},{5,1},{9,5},{13... | collective-permute-start | bytes 393224 | tf_op jit(solution)/shard_map/ppermute | solution.py:25
  9.0 14.5 %collective-permute-start.4 = (bf16[2,1,128,256]{3,2,1,0:T(8,128)(2,1)}, bf16[2,1,128,256]{3,2,1,0:T(8,128)(2,1)S(1)}, u32[]{:S(2)}, u32[]{:S(2)}) collective-permute-start(bf16[2,1,128,256]{3,2,1,0:T(8,128)(2,1)} %get-tuple-element.31), channel_id=1, source_target_pairs={{0,4},{4,8},{8,12},{12,16},{16,20},{20,24},{24,28},{1,5},{5,9},{9,... | collective-permute-start | bytes 393224 | tf_op jit(solution)/shard_map/ppermute | solution.py:23
  11.2 12.3 %collective-permute-start.5 = (bf16[2,1,128,256]{3,2,1,0:T(8,128)(2,1)}, bf16[2,1,128,256]{3,2,1,0:T(8,128)(2,1)S(1)}, u32[]{:S(2)}, u32[]{:S(2)}) collective-permute-start(bf16[2,1,128,256]{3,2,1,0:T(8,128)(2,1)} %get-tuple-element.30), channel_id=1, source_target_pairs={{4,0},{8,4},{12,8},{16,12},{20,16},{24,20},{28,24},{5,1},{9,5},{13... | collective-permute-start | bytes 393224 | tf_op jit(solution)/shard_map/ppermute | solution.py:25
  16.0 6.3 %copy-start.6 = (bf16[3,3,256,256]{3,2,1,0:T(8,128)(2,1)S(1)}, bf16[3,3,256,256]{3,2,1,0:T(8,128)(2,1)}, u32[]{:S(2)}) copy-start(bf16[3,3,256,256]{3,2,1,0:T(8,128)(2,1)} %param.6) | copy-start | bytes 3538948
  16.7 29.6 %collective-permute-start.2 = (bf16[2,14,1,256]{3,2,1,0:T(2,128)(2,1)S(1)}, bf16[2,14,1,256]{3,2,1,0:T(2,128)(2,1)S(1)}, u32[]{:S(2)}, u32[]{:S(2)}) collective-permute-start(bf16[2,14,1,256]{3,2,1,0:T(2,128)(2,1)S(1)} %get-tuple-element.25), channel_id=1, source_target_pairs={{0,1},{1,2},{2,3},{4,5},{5,6},{6,7},{8,9},{9,10},{10,11},{12,13},{... | collective-permute-start | bytes 43016 | tf_op jit(solution)/shard_map/ppermute | solution.py:23
  18.0 28.3 %collective-permute-start.3 = (bf16[2,14,1,256]{3,2,1,0:T(2,128)(2,1)S(1)}, bf16[2,14,1,256]{3,2,1,0:T(2,128)(2,1)S(1)}, u32[]{:S(2)}, u32[]{:S(2)}) collective-permute-start(bf16[2,14,1,256]{3,2,1,0:T(2,128)(2,1)S(1)} %get-tuple-element.26), channel_id=1, source_target_pairs={{1,0},{2,1},{3,2},{5,4},{6,5},{7,6},{9,8},{10,9},{11,10},{13,12},{... | collective-permute-start | bytes 43016 | tf_op jit(solution)/shard_map/ppermute | solution.py:25
  22.9 1.4 %copy-start.1 = (bf16[2,12,128,256]{3,2,1,0:T(8,128)(2,1)S(1)}, bf16[2,12,128,256]{3,2,1,0:T(8,128)(2,1)}, u32[]{:S(2)}) copy-start(bf16[2,12,128,256]{3,2,1,0:T(8,128)(2,1)} %param.5) | copy-start | bytes 4718596
  25.0 6.7 %collective-permute-start.6 = (bf16[2,14,1,256]{3,2,1,0:T(2,128)(2,1)S(1)}, bf16[2,14,1,256]{3,2,1,0:T(2,128)(2,1)S(1)}, u32[]{:S(2)}, u32[]{:S(2)}) collective-permute-start(bf16[2,14,1,256]{3,2,1,0:T(2,128)(2,1)S(1)} %get-tuple-element.20), channel_id=1, source_target_pairs={{0,1},{1,2},{2,3},{4,5},{5,6},{6,7},{8,9},{9,10},{10,11},{12,13},{... | collective-permute-start | bytes 43016 | tf_op jit(solution)/shard_map/ppermute | solution.py:23
  26.3 5.4 %collective-permute-start.7 = (bf16[2,14,1,256]{3,2,1,0:T(2,128)(2,1)S(1)}, bf16[2,14,1,256]{3,2,1,0:T(2,128)(2,1)S(1)}, u32[]{:S(2)}, u32[]{:S(2)}) collective-permute-start(bf16[2,14,1,256]{3,2,1,0:T(2,128)(2,1)S(1)} %get-tuple-element.21), channel_id=1, source_target_pairs={{1,0},{2,1},{3,2},{5,4},{6,5},{7,6},{9,8},{10,9},{11,10},{13,12},{... | collective-permute-start | bytes 43016 | tf_op jit(solution)/shard_map/ppermute | solution.py:25
  39.8 0.7 copy-start.7
  43.5 61.2 %collective-permute-start.8 = (bf16[2,12,128,256]{2,3,1,0:T(8,128)(2,1)}, bf16[2,12,128,256]{2,3,1,0:T(8,128)(2,1)}, u32[]{:S(2)}, u32[]{:S(2)}) collective-permute-start(bf16[2,12,128,256]{2,3,1,0:T(8,128)(2,1)} %convolution_bitcast_fusion), channel_id=1, source_target_pairs={{0,1},{2,3},{4,5},{6,7},{8,9},{10,11},{12,13},{14,15},{16,17},{18,... | collective-permute-start | bytes 4718600 | tf_op jit(solution)/shard_map/ppermute | solution.py:148
  44.8 37.5 %collective-permute-start.9 = (bf16[2,12,128,256]{2,3,1,0:T(8,128)(2,1)}, bf16[2,12,128,256]{2,3,1,0:T(8,128)(2,1)}, u32[]{:S(2)}, u32[]{:S(2)}) collective-permute-start(bf16[2,12,128,256]{2,3,1,0:T(8,128)(2,1)} %convolution_bitcast_fusion), channel_id=1, source_target_pairs={{0,2},{1,3},{4,6},{5,7},{8,10},{9,11},{12,14},{13,15},{16,18},{17,... | collective-permute-start | bytes 4718600 | tf_op jit(solution)/shard_map/ppermute | solution.py:35
  82.3 22.4 %collective-permute-start.10 = (bf16[2,12,128,256]{2,3,1,0:T(8,128)(2,1)}, bf16[2,12,128,256]{2,3,1,0:T(8,128)(2,1)}, u32[]{:S(2)}, u32[]{:S(2)}) collective-permute-start(bf16[2,12,128,256]{2,3,1,0:T(8,128)(2,1)} %collective-permute-done.9), channel_id=1, source_target_pairs={{1,0},{3,2},{5,4},{7,6},{9,8},{11,10},{13,12},{15,14},{17,16},{19,... | collective-permute-start | bytes 4718600 | tf_op jit(solution)/shard_map/ppermute | solution.py:149
  93.0 3.1 %copy-start.5 = (bf16[2,12,128,256]{3,2,1,0:T(8,128)(2,1)S(1)}, bf16[2,12,128,256]{3,2,1,0:T(8,128)(2,1)}, u32[]{:S(2)}) copy-start(bf16[2,12,128,256]{3,2,1,0:T(8,128)(2,1)} %get-tuple-element.24) | copy-start | bytes 4718596
  96.2 2.0 %copy-start = (f32[3072,256]{1,0:T(8,128)S(1)}, f32[3072,256]{1,0:T(8,128)}, u32[]{:S(2)}) copy-start(f32[3072,256]{1,0:T(8,128)} %fusion.22) | copy-start | bytes 9437188
  96.2 2.4 %copy-start.3 = (bf16[2,12,128,256]{3,2,1,0:T(8,128)(2,1)S(1)}, bf16[2,12,128,256]{3,2,1,0:T(8,128)(2,1)}, u32[]{:S(2)}) copy-start(bf16[2,12,128,256]{3,2,1,0:T(8,128)(2,1)} %param.4) | copy-start | bytes 4718596
  96.2 2.9 %copy-start.4 = (bf16[2,12,128,256]{3,2,1,0:T(8,128)(2,1)S(1)}, bf16[2,12,128,256]{3,2,1,0:T(8,128)(2,1)}, u32[]{:S(2)}) copy-start(bf16[2,12,128,256]{3,2,1,0:T(8,128)(2,1)} %get-tuple-element.11) | copy-start | bytes 4718596
where the time goes:
time: 118 us; the launch traced here: 117 us
  starting transfers between devices  32.2 us (27%)
  waiting for transfers between devices  26.1 us (22%)
  matrix products  22.2 us (19%)
  other arithmetic  15.1 us (13%)
  local copies, waits for them, and re-layouts  11.8 us (10%)
  Pallas kernels  9.33 us (8%)
    ppermute x1, waiting for transfers between devices, shifted(): lax.ppermute(value, axis, [(source, source + steps) for source in range(l...  26.1 us
    dot_general x18, matrix products, encode(): jnp.dot(window, conv_weight[row_tap, col_tap], preferred_element_type=jnp...  20.4 us
    ppermute x4, starting transfers between devices, padded_2(): lax.ppermute(head, axis, [((i + 1) % count, i) for i in range(ends)])  15.6 us
    concatenate x4, other arithmetic, padded_2(): jnp.concatenate([lax.ppermute(tail, axis, [(i, (i + 1) % count) for i in...  12.8 us
    pallas_call x1, Pallas kernels, correlate(): pl.pallas_call(functools.partial(correlate_kernel, span_count, 1.0 / math...  9.33 us
    ppermute x4, starting transfers between devices, padded_2(): lax.ppermute(tail, axis, [(i, (i + 1) % count) for i in range(ends)])  7.91 us
    ppermute x1, starting transfers between devices, shards(): back = lax.ppermute(far, 'cols', [(i + 1, i) for i in pairs])  5.93 us
    slice x2, local copies, waits for them, and re-layouts, padded_2(): head = lax.slice_in_dim(cells, 0, width, axis=dim)  2.79 us
  transfers between devices with their start and end apart: 11, of which 1 were waited for; matrix products, arithmetic and copies ran while one was open for 36% of the time, Pallas kernels for 0%

commit v1 on v0

--- a/solution.py
+++ b/solution.py
@@ -12,46 +12,253 @@
 LEVELS = 4
 
 
-def padded_2(cells, sides, width):
-    for axis, dim in sides:
-        count = lax.axis_size(axis)
-        ends = count - 1
-        head = lax.slice_in_dim(cells, 0, width, axis=dim)
-        tail = lax.slice_in_dim(cells, cells.shape[dim] - width, cells.shape[dim], axis=dim)
-        cells = jnp.concatenate(
-            [
-                lax.ppermute(tail, axis, [(i, (i + 1) % count) for i in range(ends)]),
-                cells,
-                lax.ppermute(head, axis, [((i + 1) % count, i) for i in range(ends)]),
-            ],
-            axis=dim,
-        )
-    return cells
-
-
-def shifted(value, axis, steps):
-    count = lax.axis_size(axis)
-    leading, last = (max(0, -steps), min(count, count - steps))
-    return lax.ppermute(value, axis, [(source, source + steps) for source in range(leading, last)])
-
-
-def encode(padded, conv_weight, conv_bias):
-    batch = padded.shape[0]
-    height = padded.shape[1] - 2
-    breadth = padded.shape[2] - 2
-    channels = padded.shape[3]
-    total = jnp.zeros((batch * height * breadth, channels), jnp.float32)
-    for row_tap in range(3):
-        for col_tap in range(3):
-            window = padded[:, row_tap : row_tap + height, col_tap : col_tap + breadth].reshape(
-                -1, channels
+MESH = pl.DeviceIdType.MESH
+AROUND = ((-1, 0), (1, 0), (0, -1), (0, 1), (-1, -1), (-1, 1), (1, -1), (1, 1))
+OPPOSITE = (1, 0, 3, 2, 7, 6, 5, 4)
+
+
+def encode_kernel(
+    row_count, col_count, part, images, row_edges, col_edges, corners, weight_ref, bias_ref, flip_ref,
+    left_out, right_out, near, far,
+    row_halo, col_halo, corner_halo, padded, send_sem, recv_sem, far_sems, own_sems, pass_sems
+):
+    _, batch, height, breadth, channels = images.shape
+    my_row, my_col = lax.axis_index("rows"), lax.axis_index("cols")
+    parts = height // part
+    chunks = batch * parts
+
+    def inside(step_row, step_col):
+        row, col = my_row + step_row, my_col + step_col
+        return (row >= 0) & (row < row_count) & (col >= 0) & (col < col_count)
+
+    barrier = pltpu.get_barrier_semaphore()
+    partners = AROUND + ((0, -2), (0, 2))
+    for step_row, step_col in partners:
+
+        @pl.when(inside(step_row, step_col))
+        def _():
+            pl.semaphore_signal(
+                barrier, inc=1, device_id=(my_row + step_row, my_col + step_col), device_id_type=MESH
             )
-            total = total + jnp.dot(
-                window, conv_weight[row_tap, col_tap], preferred_element_type=jnp.float32
-            )
-    centre = padded[:, 1:-1, 1:-1].reshape(-1, channels).astype(jnp.float32)
-    encoded = centre + jax.nn.relu(total + conv_bias)
-    return encoded.astype(jnp.bfloat16).reshape(batch, height, breadth, channels)
+
+    peers = sum(inside(*step).astype(jnp.int32) for step in partners)
+    pl.semaphore_wait(barrier, peers)
+
+    def halo(side):
+        if side < 2:
+            return row_edges.at[side], row_halo
+        if side < 4:
+            return col_edges.at[side - 2], col_halo
+        return corners.at[side - 4], corner_halo
+
+    def halo_copy(side):
+        first = 0 if side < 2 else 2 if side < 4 else 4
+        source, target = halo(side)
+        there = OPPOSITE[side]
+        return pltpu.make_async_remote_copy(
+            src_ref=source, dst_ref=target.at[there - first],
+            send_sem=send_sem.at[side], recv_sem=recv_sem.at[there],
+            device_id=(my_row + AROUND[side][0], my_col + AROUND[side][1]), device_id_type=MESH,
+        )
+
+    for side in range(8):
+        there = inside(*AROUND[side])
+
+        @pl.when(there)
+        def _():
+            halo_copy(side).start()
+
+        @pl.when(jnp.logical_not(there))
+        def _():
+            first = 0 if side < 2 else 2 if side < 4 else 4
+            target = halo(side)[1]
+            target[side - first] = jnp.zeros(target.shape[1:], target.dtype)
+
+    has_far = my_col >= 2
+    odd = lax.rem(my_col, 2) == 1
+    has_near = odd | has_far
+
+    @pl.when(jnp.logical_not(has_far))
+    def _():
+        far[...] = jnp.zeros_like(far)
+
+    @pl.when(jnp.logical_not(has_near))
+    def _():
+        near[...] = jnp.zeros_like(near)
+
+    for side in range(8):
+
+        @pl.when(inside(*AROUND[OPPOSITE[side]]))
+        def _():
+            halo_copy(side).wait_recv()
+
+    column = lax.broadcasted_iota(jnp.int32, (breadth, 1), 0)
+
+    def place(image, b, line, row, before, after):
+        wide = row.astype(jnp.float32)
+        right = jnp.where(column == 0, before.astype(jnp.float32), pltpu.roll(wide, 1, 0))
+        left = jnp.where(
+            column == breadth - 1, after.astype(jnp.float32), pltpu.roll(wide, breadth - 1, 0)
+        )
+        padded[image, b, line] = jnp.concatenate(
+            [right.astype(jnp.bfloat16), row, left.astype(jnp.bfloat16)], axis=1
+        )
+
+    def prepare(image):
+        for b in range(batch):
+            for edge in range(2):
+                place(
+                    image, b, edge * (height + 1), row_halo[edge, image, b],
+                    corner_halo[2 * edge, image, b], corner_halo[2 * edge + 1, image, b],
+                )
+
+            def line(h, carry):
+                place(
+                    image, b, h + 1, images[image, b, h],
+                    col_halo[0, image, b, h], col_halo[1, image, b, h],
+                )
+                return carry
+
+            lax.fori_loop(0, height, line, 0)
+
+    def encoded(image, b, h):
+        total = bias_ref[...]
+        for tap in range(3):
+            window = padded[image, b, pl.ds(h + tap, part)].reshape(part * breadth, 3 * channels)
+            product = jnp.dot(window, weight_ref[tap], preferred_element_type=jnp.float32)
+            total = product + total
+        centre = images[image, b, pl.ds(h, part)].reshape(part * breadth, channels)
+        out = centre.astype(jnp.float32) + jnp.maximum(total, 0.0)
+        return out.astype(jnp.bfloat16).reshape(part, breadth, channels)
+
+    def far_copy(i):
+        rows = pl.ds(i * part, part)
+        return pltpu.make_async_remote_copy(
+            src_ref=right_out.at[rows], dst_ref=far.at[rows],
+            send_sem=far_sems.at[0, i], recv_sem=far_sems.at[1, i],
+            device_id=(my_row, my_col + 2), device_id_type=MESH,
+        )
+
+    def own_copy(i):
+        rows = pl.ds(i * part, part)
+        return pltpu.make_async_remote_copy(
+            src_ref=right_out.at[rows], dst_ref=near.at[rows],
+            send_sem=own_sems.at[0, i], recv_sem=own_sems.at[1, i],
+            device_id=(my_row, my_col + 1), device_id_type=MESH,
+        )
+
+    def pass_copy(i):
+        rows = pl.ds(i * part, part)
+        return pltpu.make_async_remote_copy(
+            src_ref=far.at[rows], dst_ref=near.at[rows],
+            send_sem=pass_sems.at[0, i], recv_sem=pass_sems.at[1, i],
+            device_id=(my_row, my_col - 1), device_id_type=MESH,
+        )
+
+    sends_far = my_col + 2 < col_count
+    even = jnp.logical_not(odd)
+    prepare(1)
+
+    def right_chunk(i, carry):
+        enc = encoded(1, i // parts, (i % parts) * part)
+        for row in range(part):
+            turned = jnp.dot(flip_ref[...], enc[row], preferred_element_type=jnp.float32)
+            right_out[i * part + row] = turned.astype(jnp.bfloat16)
+
+        @pl.when(sends_far)
+        def _():
+            far_copy(i).start()
+
+        @pl.when(even)
+        def _():
+            own_copy(i).start()
+
+        return carry
+
+    lax.fori_loop(0, chunks, right_chunk, 0)
+    prepare(0)
+
+    def left_chunk(i, carry):
+        left_out[pl.ds(i * part, part)] = encoded(0, i // parts, (i % parts) * part)
+        return carry
+
+    lax.fori_loop(0, chunks, left_chunk, 0)
+
+    def arrive(i, carry):
+        @pl.when(has_far)
+        def _():
+            far_copy(i).wait_recv()
+
+        @pl.when(has_far & odd)
+        def _():
+            pass_copy(i).start()
+
+        return carry
+
+    lax.fori_loop(0, chunks, arrive, 0)
+
+    def finish(i, carry):
+        @pl.when(odd)
+        def _():
+            own_copy(i).wait_recv()
+
+        @pl.when(has_far & even)
+        def _():
+            pass_copy(i).wait_recv()
+
+        @pl.when(has_far & odd)
+        def _():
+            pass_copy(i).wait_send()
+
+        @pl.when(sends_far)
+        def _():
+            far_copy(i).wait_send()
+
+        @pl.when(even)
+        def _():
+            own_copy(i).wait_send()
+
+        return carry
+
+    lax.fori_loop(0, chunks, finish, 0)
+    for side in range(8):
+
+        @pl.when(inside(*AROUND[side]))
+        def _():
+            halo_copy(side).wait_send()
+
+
+def encode(left_features, right_features, conv_weight, conv_bias):
+    batch, height, breadth, channels = left_features.shape
+    images = jnp.stack([left_features, right_features])
+    row_edges = jnp.stack([images[:, :, 0], images[:, :, -1]])
+    col_edges = jnp.stack([images[:, :, :, :1], images[:, :, :, -1:]])
+    corners = jnp.stack(
+        [images[:, :, r, c : c + 1] for r in (0, height - 1) for c in (0, breadth - 1)]
+    )
+    weight = conv_weight.reshape(3, 3 * channels, channels)
+    flip = jnp.eye(breadth, dtype=jnp.bfloat16)[::-1]
+    part = math.gcd(height, 4)
+    chunks = batch * height // part
+    flat = jax.ShapeDtypeStruct((batch * height, breadth, channels), jnp.bfloat16)
+    vmem = pl.BlockSpec(memory_space=pltpu.VMEM)
+    dma = pltpu.SemaphoreType.DMA
+    return pl.pallas_call(
+        functools.partial(encode_kernel, lax.axis_size("rows"), lax.axis_size("cols"), part),
+        out_shape=[flat] * 4,
+        in_specs=[vmem] * 7,
+        out_specs=[vmem] * 4,
+        scratch_shapes=[
+            pltpu.VMEM(row_edges.shape, jnp.bfloat16),
+            pltpu.VMEM(col_edges.shape, jnp.bfloat16),
+            pltpu.VMEM(corners.shape, jnp.bfloat16),
+            pltpu.VMEM((2, batch, height + 2, breadth, 3 * channels), jnp.bfloat16),
+            dma((8,)), dma((8,)), dma((2, chunks)), dma((2, chunks)), dma((2, chunks)),
+        ],
+        compiler_params=pltpu.CompilerParams(
+            collective_id=0, has_side_effects=True, vmem_limit_bytes=60 * 2**20
+        ),
+    )(images, row_edges, col_edges, corners, weight, conv_bias.reshape(1, -1), flip)
 
 
 def pooling(span_count, level_count):
@@ -132,30 +339,11 @@
 
 def shards(left_features, right_features, conv_weight, conv_bias):
     batch, height, breadth, channels = left_features.shape
-    left_pad, right_pad = (
-        padded_2(left_features, (("rows", 1), ("cols", 2)), 1),
-        padded_2(right_features, (("rows", 1), ("cols", 2)), 1),
-    )
-    left_out = encode(left_pad, conv_weight, conv_bias)
-    right_out = encode(right_pad, conv_weight, conv_bias)
-    flip = jnp.eye(breadth, dtype=jnp.bfloat16)[::-1]
-    right_out = jnp.einsum("xy,bhyc->bhxc", flip, right_out)
-    hops = DISP // breadth
     count = lax.axis_size("cols")
-    if hops == 2 and count % 2 == 0:
-        far = shifted(right_out, "cols", 2)
-        pairs = range(0, count, 2)
-        own = lax.ppermute(right_out, "cols", [(i, i + 1) for i in pairs])
-        back = lax.ppermute(far, "cols", [(i + 1, i) for i in pairs])
-        odd = lax.rem(lax.axis_index("cols"), 2) == 1
-        pieces = [right_out, jnp.where(odd, own, back), far]
-    else:
-        pieces = [right_out] + [shifted(right_out, "cols", step) for step in range(1, hops + 1)]
+    assert 2 * breadth == DISP and count % 2 == 0
+    left, right, near, far = encode(left_features, right_features, conv_weight, conv_bias)
     rows_total = batch * height
-    flat = [piece.reshape(rows_total, breadth, channels) for piece in pieces]
-    out = correlate(
-        left_out.reshape(rows_total, breadth, channels), flat, DISP, LEVELS, math.gcd(rows_total, 4)
-    )
+    out = correlate(left, [right, near, far], DISP, LEVELS, math.gcd(rows_total, 4))
     return jnp.swapaxes(out, 1, 2).reshape(batch, height, breadth, -1)
 
 

time: 118 us -> 76.1 us (0.64)
  Pallas kernels: 9.33 us -> 68.9 us
  starting transfers between devices: 32.2 us -> 0 us
  waiting for transfers between devices: 26.1 us -> 0 us
  matrix products: 22.2 us -> 0 us
  local copies, waits for them, and re-layouts: 11.8 us -> 0.76 us
  other arithmetic: 15.1 us -> 6.06 us
    pallas_call x0 -> x1, Pallas kernels: none -> 59.6 us  [encode(): pl.pallas_call(functools.partial(encode_kernel, lax.axis_size('rows'), la...]
    ppermute x11 -> x0, starting transfers between devices: 32.2 us -> none  [the longest x4 15.6 us: padded_2(): lax.ppermute(head, axis, [((i + 1) % count, i) for i in range(ends)])]
    ppermute x11 -> x0, waiting for transfers between devices: 26.1 us -> none  [the longest x1 26.1 us: shifted(): lax.ppermute(value, axis, [(source, source + steps) for source in range(l...]
    dot_general x19 -> x0, matrix products: 22.2 us -> none  [the longest x18 20.4 us: encode(): jnp.dot(window, conv_weight[row_tap, col_tap], preferred_element_type=jnp...]
    concatenate x4 -> x0, other arithmetic: 12.8 us -> none  [padded_2(): jnp.concatenate([lax.ppermute(tail, axis, [(i, (i + 1) % count) for i in...]
    another operation x3 -> x10, other arithmetic: 0.04 us -> 5.38 us  [the longest x2 2.05 us: encode(): images = jnp.stack([left_features, right_features])]
    slice x4 -> x0, local copies, waits for them, and re-layouts: 2.89 us -> none  [the longest x2 2.79 us: padded_2(): head = lax.slice_in_dim(cells, 0, width, axis=dim)]
    ppermute x1 -> x0, local copies, waits for them, and re-layouts: 2.59 us -> none  [shifted(): lax.ppermute(value, axis, [(source, source + steps) for source in range(l...]
  transfers between devices with their start and end apart: 11 -> 0, of which waited for: 1 -> 0; matrix products, arithmetic and copies ran while one was open for 36% -> 0% of each run, Pallas kernels for 0% -> 0%
where the time goes in v1:
time: 76.1 us; the launch traced here: 75.8 us
  Pallas kernels  68.9 us (91%)
  other arithmetic  6.06 us (8%)
    pallas_call x1, Pallas kernels, encode(): pl.pallas_call(functools.partial(encode_kernel, lax.axis_size('rows'), la...  59.6 us
    pallas_call x1, Pallas kernels, correlate(): pl.pallas_call(functools.partial(correlate_kernel, span_count, 1.0 / math...  9.35 us
    another operation x2, other arithmetic, encode(): images = jnp.stack([left_features, right_features])  2.05 us
    another operation x2, other arithmetic, encode(): jnp.stack([images[:, :, r, c:c + 1] for r in (0, height - 1) for c in (0,...  1.61 us

profile of v1, /device:TPU:21, one launch (start us, length us, event | category | flops | bytes accessed | tf_op | source)
XLA Modules:
  0.0 75.8 jit_solution(4617205093562575453)
XLA Ops:
  0.0 0.0 copy-start
  0.0 0.0 copy-start.1
  0.0 1.0 %fusion.14 = (bf16[1,2,2,1,256]{4,3,2,1,0:T(2,128)(2,1)S(1)}, bf16[1,2,2,1,256]{4,3,2,1,0:T(2,128)(2,1)S(1)}, bf16[1,2,2,1,256]{4,3,2,1,0:T(2,128)(2,1)S(1)}, bf16[1,2,2,1,256]{4,3,2,1,0:T(2,128)(2,1)S(1)}) fusion(bf16[1,2,12,128,256]{4,3,2,1,0:T(8,128)(2,1)} %bitcast.23, bf16[1,2,12,128,256]{4,3,2,1,0:T(8,128)(2,1)} %bitcast.27), kind=kLoop, calls=%fused_computation.44 | loop fusion | flops 4096 | bytes 3153920 | tf_op jit(solution)/shard_map/stack;squeeze | solution.py:236
  1.0 0.6 pad_maximum_fusion.4.corners
  1.7 0.6 rev.3.flip_ref
  2.3 0.7 pad_maximum_fusion.2.refs_3_
  3.0 0.0 copy-done
  3.0 0.0 copy-done.1
  3.0 0.1 fusion.5
  3.1 0.1 copy_bitcast_fusion
  3.3 0.8 %pad_maximum_fusion.3.col_edges = bf16[2,2,2,12,1,256]{5,4,3,2,1,0:T(2,128)(2,1)} fusion(bf16[1,2,2,12,1,256]{5,4,3,2,1,0:T(2,128)(2,1)S(1)} %copy.66, bf16[1,2,2,12,1,256]{5,4,3,2,1,0:T(2,128)(2,1)S(1)} %copy.65), kind=kLoop, calls=%fused_computation.25 | loop fusion | flops 24576 | bytes 98304 | tf_op jit(solution)/shard_map/stack | solution.py:235
  4.1 0.9 %pad_maximum_fusion.1.row_edges = bf16[2,2,2,128,256]{4,3,2,1,0:T(8,128)(2,1)} fusion(bf16[1,2,2,128,256]{4,3,2,1,0:T(8,128)(2,1)S(1)} %get-tuple-element.20, bf16[1,2,2,128,256]{4,3,2,1,0:T(8,128)(2,1)S(1)} %get-tuple-element.19), kind=kLoop, calls=%fused_computation.17 | loop fusion | flops 262144 | bytes 1048576 | tf_op jit(solution)/shard_map/stack | solution.py:234
  5.0 1.9 %pad_maximum_fusion.images = bf16[2,2,12,128,256]{4,3,2,1,0:T(8,128)(2,1)} fusion(bf16[1,2,12,128,256]{4,3,2,1,0:T(8,128)(2,1)S(1)} %bitcast.26, bf16[1,2,12,128,256]{4,3,2,1,0:T(8,128)(2,1)S(1)} %bitcast.30), kind=kLoop, calls=%fused_computation.8 | loop fusion | flops 1572864 | bytes 6291456 | tf_op jit(solution)/shard_map/stack | solution.py:233
  6.9 59.6 %shard_map.46 = (bf16[24,128,256]{2,1,0:T(8,128)(2,1)}, bf16[24,128,256]{2,1,0:T(8,128)(2,1)}, bf16[24,128,256]{2,1,0:T(8,128)(2,1)}, bf16[24,128,256]{2,1,0:T(8,128)(2,1)}) custom-call(bf16[2,2,12,128,256]{4,3,2,1,0:T(8,128)(2,1)} %pad_maximum_fusion.images, bf16[2,2,2,128,256]{4,3,2,1,0:T(8,128)(2,1)} %pad_maximum_fusion.1.row_edges, ...), custom_call_target="tpu_custom_call" | custom-call | tf_op jit(solution)/shard_map/pallas_call | solution.py:246
  66.5 9.3 %shard_map.47 = f32[24,480,128]{2,1,0:T(8,128)} custom-call(bf16[24,128,256]{2,1,0:T(8,128)(2,1)} %get-tuple-element.9.left_ref, bf16[24,128,256]{2,1,0:T(8,128)(2,1)} %get-tuple-element.10.refs_0_, bf16[24,128,256]{2,1,0:T(8,128)(2,1)} %get-tuple-element.11.refs_1_, bf16[24,128,256]{2,1,0:T(8,128)(2,1)} %get-tuple-element.12.refs_2_, ...), custom_call_target="tpu_custom_call" | custom-call | flops 1409286144 | bytes 12189696 | tf_op jit(solution)/shard_map/pallas_call | solution.py:325
  (10 shorter events, 0.2 us)
Async XLA Ops:
  0.0 3.0 %copy-start = (bf16[2,12,128,256]{3,2,1,0:T(8,128)(2,1)S(1)}, bf16[2,12,128,256]{3,2,1,0:T(8,128)(2,1)}, u32[]{:S(2)}) copy-start(bf16[2,12,128,256]{3,2,1,0:T(8,128)(2,1)} %param.5) | copy-start | bytes 4718596
  0.0 3.0 %copy-start.1 = (bf16[2,12,128,256]{3,2,1,0:T(8,128)(2,1)S(1)}, bf16[2,12,128,256]{3,2,1,0:T(8,128)(2,1)}, u32[]{:S(2)}) copy-start(bf16[2,12,128,256]{3,2,1,0:T(8,128)(2,1)} %param.4) | copy-start | bytes 4718596

commit v2 on v1

--- a/solution.py
+++ b/solution.py
@@ -3,6 +3,7 @@
 
 import jax
 import jax.numpy as jnp
+import numpy as np
 from jax import lax
 from jax.experimental import pallas as pl
 from jax.experimental.pallas import tpu as pltpu
@@ -18,11 +19,12 @@
 
 
 def encode_kernel(
-    row_count, col_count, part, images, row_edges, col_edges, corners, weight_ref, bias_ref, flip_ref,
+    row_count, col_count, part, left_in, right_in, row_edges, col_edges, corners, weight_ref, bias_ref, flip_ref,
     left_out, right_out, near, far,
     row_halo, col_halo, corner_halo, padded, send_sem, recv_sem, far_sems, own_sems, pass_sems
 ):
-    _, batch, height, breadth, channels = images.shape
+    batch, height, breadth, channels = left_in.shape
+    images = (left_in, right_in)
     my_row, my_col = lax.axis_index("rows"), lax.axis_index("cols")
     parts = height // part
     chunks = batch * parts
@@ -114,7 +116,7 @@
 
             def line(h, carry):
                 place(
-                    image, b, h + 1, images[image, b, h],
+                    image, b, h + 1, images[image][b, h],
                     col_halo[0, image, b, h], col_halo[1, image, b, h],
                 )
                 return carry
@@ -127,7 +129,7 @@
             window = padded[image, b, pl.ds(h + tap, part)].reshape(part * breadth, 3 * channels)
             product = jnp.dot(window, weight_ref[tap], preferred_element_type=jnp.float32)
             total = product + total
-        centre = images[image, b, pl.ds(h, part)].reshape(part * breadth, channels)
+        centre = images[image][b, pl.ds(h, part)].reshape(part * breadth, channels)
         out = centre.astype(jnp.float32) + jnp.maximum(total, 0.0)
         return out.astype(jnp.bfloat16).reshape(part, breadth, channels)
 
@@ -230,14 +232,23 @@
 
 def encode(left_features, right_features, conv_weight, conv_bias):
     batch, height, breadth, channels = left_features.shape
-    images = jnp.stack([left_features, right_features])
-    row_edges = jnp.stack([images[:, :, 0], images[:, :, -1]])
-    col_edges = jnp.stack([images[:, :, :, :1], images[:, :, :, -1:]])
+    pair = (left_features, right_features)
+    row_edges = jnp.stack([jnp.stack([image[:, r] for image in pair]) for r in (0, -1)])
+    col_edges = jnp.stack(
+        [
+            jnp.stack([image[:, :, c : c + 1] for image in pair])
+            for c in (0, breadth - 1)
+        ]
+    )
     corners = jnp.stack(
-        [images[:, :, r, c : c + 1] for r in (0, height - 1) for c in (0, breadth - 1)]
+        [
+            jnp.stack([image[:, r, c : c + 1] for image in pair])
+            for r in (0, height - 1)
+            for c in (0, breadth - 1)
+        ]
     )
     weight = conv_weight.reshape(3, 3 * channels, channels)
-    flip = jnp.eye(breadth, dtype=jnp.bfloat16)[::-1]
+    flip = jnp.asarray(np.eye(breadth)[::-1], dtype=jnp.bfloat16)
     part = math.gcd(height, 4)
     chunks = batch * height // part
     flat = jax.ShapeDtypeStruct((batch * height, breadth, channels), jnp.bfloat16)
@@ -246,7 +257,7 @@
     return pl.pallas_call(
         functools.partial(encode_kernel, lax.axis_size("rows"), lax.axis_size("cols"), part),
         out_shape=[flat] * 4,
-        in_specs=[vmem] * 7,
+        in_specs=[vmem] * 8,
         out_specs=[vmem] * 4,
         scratch_shapes=[
             pltpu.VMEM(row_edges.shape, jnp.bfloat16),
@@ -258,16 +269,16 @@
         compiler_params=pltpu.CompilerParams(
             collective_id=0, has_side_effects=True, vmem_limit_bytes=60 * 2**20
         ),
-    )(images, row_edges, col_edges, corners, weight, conv_bias.reshape(1, -1), flip)
+    )(left_features, right_features, row_edges, col_edges, corners, weight, conv_bias.reshape(1, -1), flip)
 
 
 def pooling(span_count, level_count):
     lines = []
-    entry = lax.broadcasted_iota(jnp.int32, (1, span_count), 1)
+    entry = np.arange(span_count)[None, :]
     for level in range(1, level_count):
-        group = lax.broadcasted_iota(jnp.int32, (span_count >> level, 1), 0)
-        lines.append(jnp.where((entry >> level) == group, 0.5**level, 0.0))
-    return jnp.concatenate(lines, axis=0).astype(jnp.bfloat16)
+        group = np.arange(span_count >> level)[:, None]
+        lines.append(np.where((entry >> level) == group, 0.5**level, 0.0))
+    return jnp.asarray(np.concatenate(lines, axis=0), dtype=jnp.bfloat16)
 
 
 def skewed(scores, span_count, scratch):

time: 76.1 us -> 77.5 us (1.018)
  local copies, waits for them, and re-layouts: 0.76 us -> 5.64 us
  other arithmetic: 6.06 us -> 2.42 us
    slice x0 -> x4, local copies, waits for them, and re-layouts: none -> 3.49 us  [the longest x2 1.97 us: encode(): image[:, :, c:c + 1]]
    another operation x10, other arithmetic: 5.38 us -> 2.42 us  [the longest x2 0.89 us: encode(): jnp.stack([jnp.stack([image[:, r] for image in pair]) for r in (0, -1)])]
    another operation x3 -> x12, local copies, waits for them, and re-layouts: 0.13 us -> 2.14 us  [the longest x2 1.98 us: encode(): jnp.stack([image[:, r] for image in pair])]
where the time goes in v2:
time: 77.5 us; the launch traced here: 77.1 us
  Pallas kernels  68.9 us (89%)
  local copies, waits for them, and re-layouts  5.64 us (7%)
  other arithmetic  2.42 us (3%)
    pallas_call x1, Pallas kernels, encode(): pl.pallas_call(functools.partial(encode_kernel, lax.axis_size('rows'), la...  59.5 us
    pallas_call x1, Pallas kernels, correlate(): pl.pallas_call(functools.partial(correlate_kernel, span_count, 1.0 / math...  9.35 us
    another operation x2, local copies, waits for them, and re-layouts, encode(): jnp.stack([image[:, r] for image in pair])  1.98 us
    slice x2, local copies, waits for them, and re-layouts, encode(): image[:, :, c:c + 1]  1.97 us

profile of v2, /device:TPU:21, one launch (start us, length us, event | category | flops | bytes accessed | tf_op | source)
XLA Modules:
  0.0 77.1 jit_solution(11506136390722991215)
XLA Ops:
  0.0 0.8 fusion
  0.8 0.8 fusion.1
  1.7 0.6 pad_maximum_fusion.2.corners
  2.3 1.0 %fusion.2 = (bf16[2,12,1,256]{3,2,1,0:T(2,128)(2,1)S(1)}, bf16[2,12,1,256]{3,2,1,0:T(2,128)(2,1)S(1)}) fusion(bf16[2,12,128,256]{3,2,1,0:T(8,128)(2,1)} %left_in.1), kind=kLoop, calls=%fused_computation.29 | loop fusion | bytes 49152 | tf_op jit(solution)/shard_map/slice | solution.py:239
  3.3 1.0 %fusion.3 = (bf16[2,12,1,256]{3,2,1,0:T(2,128)(2,1)S(1)}, bf16[2,12,1,256]{3,2,1,0:T(2,128)(2,1)S(1)}) fusion(bf16[2,12,128,256]{3,2,1,0:T(8,128)(2,1)} %right_in.1), kind=kLoop, calls=%fused_computation.30 | loop fusion | bytes 49152 | tf_op jit(solution)/shard_map/slice | solution.py:239
  4.6 0.8 %pad_maximum_fusion.1.col_edges = bf16[2,2,2,12,1,256]{5,4,3,2,1,0:T(2,128)(2,1)} fusion(bf16[1,2,2,12,1,256]{5,4,3,2,1,0:T(2,128)(2,1)S(1)} %copy.50, bf16[1,2,2,12,1,256]{5,4,3,2,1,0:T(2,128)(2,1)S(1)} %copy.49), kind=kLoop, calls=%fused_computation.7 | loop fusion | flops 24576 | bytes 98304 | tf_op jit(solution)/shard_map/stack | solution.py:237
  5.3 1.0 %slice_bitcast_fusion.3 = (bf16[1,2,128,256]{3,2,1,0:T(8,128)(2,1)S(1)}, bf16[1,2,128,256]{3,2,1,0:T(8,128)(2,1)S(1)}) fusion(bf16[2,12,128,256]{3,2,1,0:T(8,128)(2,1)} %left_in.1), kind=kLoop, calls=%fused_computation.6 | loop fusion | bytes 524288 | tf_op jit(solution)/shard_map/stack;squeeze | solution.py:236
  6.3 1.0 %slice_bitcast_fusion.2 = (bf16[1,2,128,256]{3,2,1,0:T(8,128)(2,1)S(1)}, bf16[1,2,128,256]{3,2,1,0:T(8,128)(2,1)S(1)}) fusion(bf16[2,12,128,256]{3,2,1,0:T(8,128)(2,1)} %right_in.1), kind=kLoop, calls=%fused_computation.5 | loop fusion | bytes 524288 | tf_op jit(solution)/shard_map/stack;squeeze | solution.py:236
  7.4 0.8 %pad_maximum_fusion.row_edges = bf16[2,2,2,128,256]{4,3,2,1,0:T(8,128)(2,1)} fusion(bf16[1,2,2,128,256]{4,3,2,1,0:T(8,128)(2,1)S(1)} %get-tuple-element.30, bf16[1,2,2,128,256]{4,3,2,1,0:T(8,128)(2,1)S(1)} %get-tuple-element.29), kind=kLoop, calls=%fused_computation | loop fusion | flops 262144 | bytes 1048576 | tf_op jit(solution)/shard_map/stack | solution.py:236
  8.2 59.5 %shard_map.64 = (bf16[24,128,256]{2,1,0:T(8,128)(2,1)}, bf16[24,128,256]{2,1,0:T(8,128)(2,1)}, bf16[24,128,256]{2,1,0:T(8,128)(2,1)}, bf16[24,128,256]{2,1,0:T(8,128)(2,1)}) custom-call(bf16[2,12,128,256]{3,2,1,0:T(8,128)(2,1)} %left_in.1, bf16[2,12,128,256]{3,2,1,0:T(8,128)(2,1)} %right_in.1, bf16[2,2,2,128,256]{4,3,2,1,0:T(8,128)(2,1)} %pad_maximum_fusion.row_edges, ...), custom_call_target="tpu_custom_call" | custom-call | tf_op jit(solution)/shard_map/pallas_call | solution.py:257
  67.7 9.4 %shard_map.65 = f32[24,480,128]{2,1,0:T(8,128)} custom-call(bf16[24,128,256]{2,1,0:T(8,128)(2,1)} %get-tuple-element.9.left_ref, bf16[24,128,256]{2,1,0:T(8,128)(2,1)} %get-tuple-element.10.refs_0_, bf16[24,128,256]{2,1,0:T(8,128)(2,1)} %get-tuple-element.11.refs_1_, bf16[24,128,256]{2,1,0:T(8,128)(2,1)} %get-tuple-element.12.refs_2_, ...), custom_call_target="tpu_custom_call" | custom-call | flops 1409286144 | bytes 12189696 | tf_op jit(solution)/shard_map/pallas_call | solution.py:336
  (19 shorter events, 0.3 us)
